TPU v7x, 512 devices: a 8x2x16 block of a 8x8x16 slice. The times are simulated.
512 devices in a mesh: rep: 2 (over y), exp: 16 (over x, core), tp: 16 (over z).
Axes of the slice: x: 8, y: 2, z: 16, core: 2. Of those that a mesh axis runs over, the one named last changes fastest.
The devices are a block of a 8x8x16 slice.
Arguments:
- tokens: bfloat16 [1024, 6144], P(('rep', 'exp'), 'tp'), parts along dimension 0, may hold values from -6 to 6
- expert_ids: int32 [1024, 2], P(('rep', 'exp')), parts along dimension 0, may hold values from 0 to 3, all different within a row; in each aligned block of 32 rows (0 to 31, 32 to 63, ...) at most 20 rows name the same one
- route_logits: float32 [1024, 2], P(('rep', 'exp')), parts along dimension 0, may hold values from -6 to 6
- gate_weight: bfloat16 [6144, 32768], P(None, ('exp', 'tp')), may hold values from -0.078125 to 0.078125
- up_weight: bfloat16 [6144, 32768], P(None, ('exp', 'tp')), may hold values from -0.078125 to 0.078125
- down_weight: bfloat16 [32768, 6144], P(('exp', 'tp')), may hold values from -0.0625 to 0.0625
Outputs:
- moe_out: bfloat16 [1024, 6144], P(('rep', 'exp'), 'tp'), parts along dimension 0
There are 2 independent parts, one for each index of `rep`. A program takes and returns all parts, laid end to end along the dimension named above; an argument that names none is the same for every part. Nothing has to cross between parts.
Inputs may be any that keep to these rules, and one draw needn't show every extreme that they name: `expert_ids`: each token names two different experts. In each aligned block of 32 tokens no expert is named by more than 20 tokens, a bound that some block reaches.
All inputs are finite; a program needn't handle non-finite values.
Results may differ from a plain program's by a relative error of at most 0.019.
Values may be sent and summed in bfloat16 or wider, within the bound.
No kernel may reach another device: no remote copies, remote signals or barrier semaphores. Data moves between devices by JAX's collectives and lax.ppermute only.
A program may use at most 64 MiB of HBM per device.

v0:
```python
import jax
import jax.numpy as jnp
from jax import lax
from jax.sharding import PartitionSpec as P

D = 6144
EXPERTS = 4
CAP = 20


def cut_along(x, dim, devices):
    shape = x.shape
    blocks = x.reshape(*shape[:dim], devices, shape[dim] // devices, *shape[dim + 1 :])
    return jnp.moveaxis(blocks, dim, 0)


def sum_at_owner(x, axis, dim):
    devices = lax.axis_size(axis)
    blocks = lax.all_to_all(cut_along(x, dim, devices), axis, 0, 0, tiled=True)
    return jnp.sum(blocks.astype(jnp.float32), axis=0)


def slot_tables(expert_ids, route_logits):
    chosen = (expert_ids[:, :, None] == jnp.arange(EXPERTS, dtype=jnp.int32)[None, None, :]).astype(
        jnp.int32
    )
    per_token = jnp.sum(chosen, axis=1)
    before = jnp.cumsum(per_token, axis=0) - per_token
    position = jnp.sum(chosen * before[:, None, :], axis=2)
    at_slot = (position[:, :, None] == jnp.arange(CAP, dtype=jnp.int32)[None, None, :]).astype(
        jnp.float32
    )
    chosen_f = chosen.astype(jnp.float32)
    diff = route_logits[:, 0] - route_logits[:, 1]
    shares = jnp.stack([jax.nn.sigmoid(diff), jax.nn.sigmoid(-diff)], axis=1)
    placement = jnp.einsum("tke,tkc->ect", chosen_f, at_slot)
    mixing = jnp.einsum("tk,tke,tkc->tec", shares, chosen_f, at_slot)
    return (placement.astype(jnp.bfloat16), mixing)


def on_device(tokens, expert_ids, route_logits, gate_weight, up_weight, down_weight):
    exp_count = lax.axis_size("exp")
    groups = exp_count // EXPERTS
    placement, mixing = slot_tables(expert_ids, route_logits)
    slots = jnp.einsum("ect,td->ecd", placement, tokens, preferred_element_type=jnp.float32).astype(
        jnp.bfloat16
    )
    outgoing = jnp.repeat(slots, groups, axis=0)
    incoming = lax.all_to_all(outgoing, "exp", split_axis=0, concat_axis=0, tiled=True)
    gathered = lax.all_gather(incoming, "tp", axis=2, tiled=True)
    slot_rows = gathered.reshape(exp_count * CAP, D)
    gate_act = jnp.dot(slot_rows, gate_weight, preferred_element_type=jnp.float32)
    up_act = jnp.dot(slot_rows, up_weight, preferred_element_type=jnp.float32)
    hidden = (jax.nn.silu(gate_act) * up_act).astype(jnp.bfloat16)
    partial_value = jnp.dot(hidden, down_weight, preferred_element_type=jnp.float32).astype(
        jnp.bfloat16
    )
    partial_value = lax.optimization_barrier(partial_value).reshape(exp_count, CAP, D)
    returned = lax.all_to_all(partial_value, "exp", split_axis=0, concat_axis=0, tiled=True)
    summed = jnp.sum(returned.astype(jnp.float32).reshape(EXPERTS, groups, CAP, D), axis=1)
    combined = jnp.einsum("tec,ecd->td", mixing, summed)
    moe_out = sum_at_owner(combined.astype(jnp.bfloat16), "tp", 1).astype(jnp.bfloat16)
    return moe_out


def solution(mesh):
    return jax.shard_map(
        on_device,
        mesh=mesh,
        in_specs=(
            P(("rep", "exp"), "tp"),
            P(("rep", "exp"), None),
            P(("rep", "exp"), None),
            P(None, ("exp", "tp")),
            P(None, ("exp", "tp")),
            P(("exp", "tp"), None),
        ),
        out_specs=P(("rep", "exp"), "tp"),
        check_vma=False,
    )
```

profile of v0, /device:TPU:70, one launch (start us, length us, event | category | flops | bytes accessed | tf_op | source)
XLA Modules:
  0.0 322.3 jit_solution(2993547651281507378)
XLA Ops:
  6.5 0.0 copy-start
  6.6 0.0 all-gather.2.cloned.1.call-start
  6.6 0.9 copy.12
  7.4 0.1 convert_reduce_fusion.1
  7.6 0.1 reduce_window_sum.11
  7.6 0.7 select_reduce_fusion
  8.3 0.4 fusion.2
  8.7 0.9 convolution_convert_fusion.1
  9.7 53.4 %all_to_all.15 = bf16[16,20,384]{2,1,0:T(8,128)(2,1)} all-to-all(bf16[16,20,384]{2,1,0:T(8,128)(2,1)S(1)} %bitcast.28), channel_id=1, replica_groups=mesh['rep'=2,'exp'=16,'tp'=16] {'exp'}, dimensions={0} | all-to-all | bytes 491520 | tf_op jit(solution)/shard_map/all_to_all | solution.py:49
  63.0 0.1 all-gather.2.cloned.1.call-update
  63.1 0.0 copy-start.1
  63.1 78.8 %all-gather.2.cloned.1.call-done = bf16[16,20,6144]{2,1,0:T(8,128)(2,1)} async-done(((bf16[16,20,384]{2,1,0:T(8,128)(2,1)}), bf16[16,20,6144]{2,1,0:T(8,128)(2,1)}) %all-gather.2.cloned.1.call-update) | async-done | bytes 3932176 | tf_op jit(solution)/shard_map/all_gather | solution.py:50
  141.9 7.0 %reshape.30 = bf16[320,6144]{1,0:T(8,128)(2,1)} reshape(bf16[16,20,6144]{2,1,0:T(8,128)(2,1)} %all-gather.2.cloned.1.call-done) | data formatting | bytes 7864320 | tf_op jit(solution)/shard_map/reshape | solution.py:51
  148.8 0.0 copy-done.1
  148.8 3.3 %fusion.21 = f32[320,128]{1,0:T(8,128)S(1)} fusion(bf16[320,6144]{1,0:T(8,128)(2,1)} %reshape.30, bf16[6144,128]{1,0:T(8,128)(2,1)S(1)} %copy-done.1), kind=kOutput, calls=%fused_computation.36 | convolution fusion | flops 503316480 | bytes 5668864 | tf_op jit(solution)/shard_map/dot_general | solution.py:52
  152.1 0.0 copy-done
  152.1 8.7 %convolution_convert_fusion = bf16[320,6144]{1,0:T(8,128)(2,1)} fusion(bf16[128,6144]{1,0:T(8,128)(2,1)S(1)} %copy-done, bf16[320,6144]{1,0:T(8,128)(2,1)} %reshape.30, bf16[6144,128]{1,0:T(8,128)(2,1)} %param.10, f32[320,128]{1,0:T(8,128)S(1)} %fusion.21), kind=kOutput, calls=%fused_computation.1 | convolution fusion | flops 1008844800 | bytes 11173888 | tf_op jit(solution)/shard_map/dot_general | solution.py:55
  160.9 6.9 %reshape.31 = bf16[16,20,6144]{2,1,0:T(8,128)(2,1)} reshape(bf16[320,6144]{1,0:T(8,128)(2,1)} %convolution_convert_fusion) | data formatting | bytes 7864320 | tf_op jit(solution)/shard_map/reshape | solution.py:58
  167.7 0.0 copy-start.2
  167.7 7.4 %all-to-all-start.1 = ((bf16[16,20,6144]{2,1,0:T(8,128)(2,1)}), bf16[16,20,6144]{2,1,0:T(8,128)(2,1)}, u32[]{:S(2)}, u32[]{:S(2)}) async-start(bf16[16,20,6144]{2,1,0:T(8,128)(2,1)} %reshape.31), calls=%async_computation.1 | async-start | bytes 9437184 | tf_op jit(solution)/shard_map/all_to_all | solution.py:59
  175.1 0.0 copy-done.2
  175.2 0.1 copy.11
  175.3 0.4 fusion.11
  175.7 104.4 %all-to-all-done.1 = bf16[16,20,6144]{2,1,0:T(8,128)(2,1)} async-done(((bf16[16,20,6144]{2,1,0:T(8,128)(2,1)}), bf16[16,20,6144]{2,1,0:T(8,128)(2,1)}, u32[]{:S(2)}, u32[]{:S(2)}) %all-to-all-start.1) | async-done | bytes 3932192 | tf_op jit(solution)/shard_map/all_to_all | solution.py:59
  280.1 3.2 convert_reduce_fusion
  283.3 0.5 fusion
  283.8 0.1 copy.22
  283.9 30.8 %all_to_all.16 = bf16[16,32,384]{2,1,0:T(8,128)(2,1)S(1)} all-to-all(bf16[16,32,384]{2,1,0:T(8,128)(2,1)S(1)} %bitcast.26), channel_id=1, replica_groups=mesh['rep'=2,'exp'=16,'tp'=16] {'tp'}, dimensions={0} | all-to-all | bytes 786432 | tf_op jit(solution)/shard_map/all_to_all | solution.py:19
  314.7 0.7 reduce_sum.42
  (4 shorter events, 0.1 us)
Async XLA Ops:
  6.5 145.6 %copy-start = (bf16[128,6144]{1,0:T(8,128)(2,1)S(1)}, bf16[128,6144]{1,0:T(8,128)(2,1)}, u32[]{:S(2)}) copy-start(bf16[128,6144]{1,0:T(8,128)(2,1)} %param.11) | copy-start | bytes 4718596
  6.6 135.3 %all-gather.2.cloned.1.call-start = ((), (), s32[]{:S(2)}) async-start(), calls=%async_computation.3 | async-start | bytes 5013504 | tf_op jit(solution)/shard_map/all_gather | solution.py:50
  63.1 85.8 %copy-start.1 = (bf16[6144,128]{1,0:T(8,128)(2,1)S(1)}, bf16[6144,128]{1,0:T(8,128)(2,1)}, u32[]{:S(2)}) copy-start(bf16[6144,128]{1,0:T(8,128)(2,1)} %param.9) | copy-start | bytes 4718596
  167.7 7.4 %copy-start.2 = (f32[32,2]{0,1:T(2,128)S(1)}, f32[32,2]{0,1:T(2,128)}, u32[]{:S(2)}) copy-start(f32[32,2]{0,1:T(2,128)} %param.8) | copy-start | bytes 772
  167.7 112.3 %all-to-all-start.1 = ((bf16[16,20,6144]{2,1,0:T(8,128)(2,1)}), bf16[16,20,6144]{2,1,0:T(8,128)(2,1)}, u32[]{:S(2)}, u32[]{:S(2)}) async-start(bf16[16,20,6144]{2,1,0:T(8,128)(2,1)} %reshape.31), calls=%async_computation.1 | async-start | bytes 9437184 | tf_op jit(solution)/shard_map/all_to_all | solution.py:59
Sparse Core Ops, SparseCore 0:
  63.2 78.6 all-gather.1
where the time goes:
time: 323 us; the launch traced here: 322 us
  waiting for transfers between devices  183 us (57%)
  blocking collectives  84.2 us (26%)
  local copies, waits for them, and re-layouts  14.9 us (5%)
  matrix products  14.3 us (4%)
  between operations  13.5 us (4%)
  starting transfers between devices  7.38 us (2%)
  other arithmetic  4.76 us (1%)
    all_to_all x1, waiting for transfers between devices, on_device(): lax.all_to_all(partial_value, 'exp', split_axis=0, concat_axis=0, tiled=T...  104 us
    all_gather x1, waiting for transfers between devices, on_device(): gathered = lax.all_gather(incoming, 'tp', axis=2, tiled=True)  78.8 us
    all_to_all x1, blocking collectives, on_device(): lax.all_to_all(outgoing, 'exp', split_axis=0, concat_axis=0, tiled=True)  53.4 us
    all_to_all x1, blocking collectives, sum_at_owner(): blocks = lax.all_to_all(cut_along(x, dim, devices), axis, 0, 0, tiled=True)  30.8 us
    dot_general x1, matrix products, on_device(): jnp.dot(hidden, down_weight, preferred_element_type=jnp.float32)  8.73 us
    all_to_all x1, starting transfers between devices, on_device(): lax.all_to_all(partial_value, 'exp', split_axis=0, concat_axis=0, tiled=T...  7.38 us
    reshape x1, local copies, waits for them, and re-layouts, on_device(): slot_rows = gathered.reshape(exp_count * CAP, D)  6.97 us
    reshape x1, local copies, waits for them, and re-layouts, on_device(): lax.optimization_barrier(partial_value).reshape(exp_count, CAP, D)  6.87 us
  transfers between devices with their start and end apart: 2, of which 2 were waited for; matrix products, arithmetic and copies ran while one was open for 0% of the time, Pallas kernels for 0%

commit v1 on v0

--- a/solution.py
+++ b/solution.py
@@ -47,7 +47,9 @@
     )
     outgoing = jnp.repeat(slots, groups, axis=0)
     incoming = lax.all_to_all(outgoing, "exp", split_axis=0, concat_axis=0, tiled=True)
-    gathered = lax.all_gather(incoming, "tp", axis=2, tiled=True)
+    gathered = jnp.concatenate(
+        lax.all_to_all(jnp.stack([incoming] * lax.axis_size("tp")), "tp", 0, 0), axis=2
+    )
     slot_rows = gathered.reshape(exp_count * CAP, D)
     gate_act = jnp.dot(slot_rows, gate_weight, preferred_element_type=jnp.float32)
     up_act = jnp.dot(slot_rows, up_weight, preferred_element_type=jnp.float32)

time: 323 us -> 409 us (1.27)
  blocking collectives: 84.2 us -> 267 us
  waiting for transfers between devices: 183 us -> 104 us
  between operations: 13.5 us -> 0.12 us
    all_to_all x0 -> x1, blocking collectives: none -> 184 us  [on_device(): lax.all_to_all(jnp.stack([incoming] * lax.axis_size('tp')), 'tp', 0, 0)]
    all_gather x1 -> x0, waiting for transfers between devices: 78.8 us -> none  [on_device(): gathered = lax.all_gather(incoming, 'tp', axis=2, tiled=True)]
    reshape x1, local copies, waits for them, and re-layouts: 6.97 us -> 2.34 us  [on_device(): jnp.concatenate(lax.all_to_all(jnp.stack([incoming] * lax.axis_size('tp')...]
  transfers between devices with their start and end apart: 2 -> 1, of which waited for: 2 -> 1; matrix products, arithmetic and copies ran while one was open for 0% -> 0% of each run, Pallas kernels for 0% -> 0%
where the time goes in v1:
time: 409 us; the launch traced here: 408 us
  blocking collectives  267 us (65%)
  waiting for transfers between devices  104 us (25%)
  local copies, waits for them, and re-layouts  13.9 us (3%)
  matrix products  11.7 us (3%)
  starting transfers between devices  6.81 us (2%)
  other arithmetic  4.76 us (1%)
    all_to_all x1, blocking collectives, on_device(): lax.all_to_all(jnp.stack([incoming] * lax.axis_size('tp')), 'tp', 0, 0)  184 us
    all_to_all x1, waiting for transfers between devices, on_device(): lax.all_to_all(partial_value, 'exp', split_axis=0, concat_axis=0, tiled=T...  104 us
    all_to_all x1, blocking collectives, on_device(): lax.all_to_all(outgoing, 'exp', split_axis=0, concat_axis=0, tiled=True)  52.7 us
    all_to_all x1, blocking collectives, sum_at_owner(): blocks = lax.all_to_all(cut_along(x, dim, devices), axis, 0, 0, tiled=True)  29.8 us
    dot_general x1, matrix products, on_device(): jnp.dot(hidden, down_weight, preferred_element_type=jnp.float32)  8.25 us
  transfers between devices with their start and end apart: 1, of which 1 were waited for; matrix products, arithmetic and copies ran while one was open for 0% of the time, Pallas kernels for 0%

profile of v1, /device:TPU:70, one launch (start us, length us, event | category | flops | bytes accessed | tf_op | source)
XLA Modules:
  0.0 408.4 jit_solution(4356644125129430857)
XLA Ops:
  0.0 0.0 copy-start
  0.0 0.9 copy.25
  0.9 0.1 convert_reduce_fusion.1
  1.0 0.1 reduce_window_sum.11
  1.1 0.7 select_reduce_fusion
  1.8 0.4 fusion.2
  2.1 0.9 convolution_convert_fusion.1
  3.1 52.7 %all_to_all.20 = bf16[16,20,384]{2,1,0:T(8,128)(2,1)S(1)} all-to-all(bf16[16,20,384]{2,1,0:T(8,128)(2,1)S(1)} %bitcast.36), channel_id=1, replica_groups=mesh['rep'=2,'exp'=16,'tp'=16] {'exp'}, dimensions={0} | all-to-all | bytes 491520 | tf_op jit(solution)/shard_map/all_to_all | solution.py:49
  55.8 0.5 stack.5
  56.3 184.2 %all_to_all.21 = bf16[16,16,20,384]{3,1,2,0:T(8,128)(2,1)S(1)} all-to-all(bf16[16,16,20,384]{3,1,2,0:T(8,128)(2,1)S(1)} %stack.5), channel_id=1, replica_groups=mesh['rep'=2,'exp'=16,'tp'=16] {'tp'}, dimensions={0} | all-to-all | bytes 7864320 | tf_op jit(solution)/shard_map/all_to_all | solution.py:51
  240.5 2.3 copy.28
  242.9 0.0 copy-start.2
  242.9 1.2 copy.32
  244.1 0.0 copy-start.1
  244.1 0.0 copy-start.3
  244.1 1.9 copy-done.1
  246.0 0.0 copy-done.2
  246.0 1.2 fusion.21
  247.2 0.0 copy-done
  247.2 0.0 copy-done.3
  247.2 8.3 %convolution_convert_fusion = bf16[320,6144]{1,0:T(8,128)(2,1)} fusion(bf16[128,6144]{1,0:T(8,128)(2,1)S(1)} %copy-done, bf16[320,6144]{1,0:T(8,128)(2,1)} %bitcast.31, bf16[6144,128]{1,0:T(8,128)(2,1)S(1)} %copy-done.3, f32[320,128]{1,0:T(8,128)S(1)} %fusion.21), kind=kOutput, calls=%fused_computation.1 | convolution fusion | flops 1008844800 | bytes 11173888 | tf_op jit(solution)/shard_map/dot_general | solution.py:57
  255.5 6.9 %reshape.33 = bf16[16,20,6144]{2,1,0:T(8,128)(2,1)} reshape(bf16[320,6144]{1,0:T(8,128)(2,1)} %convolution_convert_fusion) | data formatting | bytes 7864320 | tf_op jit(solution)/shard_map/reshape | solution.py:60
  262.3 6.8 %all-to-all-start.2 = ((bf16[16,20,6144]{2,1,0:T(8,128)(2,1)}), bf16[16,20,6144]{2,1,0:T(8,128)(2,1)}, u32[]{:S(2)}, u32[]{:S(2)}) async-start(bf16[16,20,6144]{2,1,0:T(8,128)(2,1)} %reshape.33), calls=%async_computation.2 | async-start | bytes 9437184 | tf_op jit(solution)/shard_map/all_to_all | solution.py:61
  269.2 0.0 copy-done.4
  269.2 0.1 copy.24
  269.3 0.4 fusion.11
  269.7 104.4 %all-to-all-done.2 = bf16[16,20,6144]{2,1,0:T(8,128)(2,1)} async-done(((bf16[16,20,6144]{2,1,0:T(8,128)(2,1)}), bf16[16,20,6144]{2,1,0:T(8,128)(2,1)}, u32[]{:S(2)}, u32[]{:S(2)}) %all-to-all-start.2) | async-done | bytes 3932192 | tf_op jit(solution)/shard_map/all_to_all | solution.py:61
  374.1 3.2 convert_reduce_fusion
  377.4 0.5 fusion
  377.9 0.1 copy.38
  377.9 29.8 %all_to_all.22 = bf16[16,32,384]{2,1,0:T(8,128)(2,1)S(1)} all-to-all(bf16[16,32,384]{2,1,0:T(8,128)(2,1)S(1)} %bitcast.34), channel_id=1, replica_groups=mesh['rep'=2,'exp'=16,'tp'=16] {'tp'}, dimensions={0} | all-to-all | bytes 786432 | tf_op jit(solution)/shard_map/all_to_all | solution.py:19
  407.8 0.7 reduce_sum.42
  (6 shorter events, 0.1 us)
Async XLA Ops:
  0.0 247.2 %copy-start = (bf16[128,6144]{1,0:T(8,128)(2,1)S(1)}, bf16[128,6144]{1,0:T(8,128)(2,1)}, u32[]{:S(2)}) copy-start(bf16[128,6144]{1,0:T(8,128)(2,1)} %param.11) | copy-start | bytes 4718596
  242.9 3.2 copy-start.2
  244.1 1.9 copy-start.1
  244.1 3.1 copy-start.3
  262.3 6.8 %copy-start.4 = (f32[32,2]{0,1:T(2,128)S(1)}, f32[32,2]{0,1:T(2,128)}, u32[]{:S(2)}) copy-start(f32[32,2]{0,1:T(2,128)} %param.8) | copy-start | bytes 772
  262.3 111.8 %all-to-all-start.2 = ((bf16[16,20,6144]{2,1,0:T(8,128)(2,1)}), bf16[16,20,6144]{2,1,0:T(8,128)(2,1)}, u32[]{:S(2)}, u32[]{:S(2)}) async-start(bf16[16,20,6144]{2,1,0:T(8,128)(2,1)} %reshape.33), calls=%async_computation.2 | async-start | bytes 9437184 | tf_op jit(solution)/shard_map/all_to_all | solution.py:61
